TPU v7x, 32 devices: a whole 2x2x4 slice. The times are simulated.
32 devices in a mesh: groups: 2 (over x), row: 16 (over z, y, core).
Axes of the slice: x: 2, y: 2, z: 4, core: 2. Of those that a mesh axis runs over, the one named last changes fastest.
Arguments:
- factor_b: bfloat16 [64, 131072], P(None, ('groups', 'row')), parts along dimension 1, may hold values from -12 to 12
- factor_c: bfloat16 [64, 131072], P(None, ('groups', 'row')), parts along dimension 1, may hold values from -12 to 12
- sample_j: int32 [262144], P(('groups', 'row')), parts along dimension 0, may hold values from 0 to 65535, as said below
- sample_k: int32 [16, 32, 512], P(None, ('groups', 'row')), parts along dimension 1, may hold values from 0 to 65535, as said below
- sample_weight: float32 [262144], P(('groups', 'row')), parts along dimension 0, may hold values from 0.5 to 3.5
- block_values: bfloat16 [32, 16, 4, 4, 128], P(('groups', 'row')), parts along dimension 0, may hold values from -24 to 24
- block_sample: int32 [32, 16, 4, 4], P(('groups', 'row')), parts along dimension 0, may hold values from 0 to 8191
- block_count: int32 [32, 16, 4, 4], P(('groups', 'row')), parts along dimension 0, may hold values from 0 to 128, as said below
Outputs:
- factor_new: bfloat16 [64, 16384], P(None, ('groups', 'row')), parts along dimension 1
- scales: float32 [128], P('groups'), parts along dimension 0
There are 2 independent parts, one for each index of `groups`. A program takes and returns all parts, laid end to end along the dimension named above; each array names one. Nothing has to cross between parts.
Inputs may be any that keep to these rules, and one draw needn't show every extreme that they name: sample_j[s] lies in rows s // 8192 * 4096 to s // 8192 * 4096 + 4095. sample_k[d, e, i] is the third-mode index of sample d * 8192 + e * 512 + i and lies in rows e * 4096 to e * 4096 + 4095. `block_count`: 0 marks an empty slot; slot [p, p, 0, 0] holds 128 for every p.
All inputs are finite; a program needn't handle non-finite values.
Results may differ from a plain program's by a relative error of at most 0.0051.
Values may be sent and summed in bfloat16 or wider, within the bound.
A program may use at most 64 MiB of HBM per device.

v0:
```python
import jax
import jax.numpy as jnp
from jax import lax
from jax.sharding import PartitionSpec as P


def shards(
    factor_b, factor_c, sample_j, sample_k, sample_weight, block_values, block_sample, block_count
):
    rank_width = factor_b.shape[0]
    device_count = lax.axis_size("row")
    device_index = lax.axis_index("row")
    b_columns = jnp.take(factor_b, sample_j - device_index * factor_b.shape[1], axis=1)
    c_local = sample_k.reshape(-1) - device_index * factor_c.shape[1]
    c_outgoing = jnp.take(factor_c, c_local, axis=1).reshape(rank_width, device_count, -1)
    c_columns = lax.all_to_all(c_outgoing, "row", split_axis=1, concat_axis=1, tiled=True).reshape(
        rank_width, -1
    )
    sketch = sample_weight[None, :] * b_columns.astype(jnp.float32) * c_columns.astype(jnp.float32)
    gram_local = jnp.dot(sketch, sketch.T, precision=lax.Precision.HIGHEST)
    live_local = jnp.sum(block_count.astype(jnp.float32))
    gram_matrix, live_total = lax.psum((gram_local, live_local), "row")
    weighted = (sample_weight[None, :] * sketch).astype(jnp.bfloat16)
    positions = lax.broadcasted_iota(jnp.int32, block_values.shape, 4)
    masked = jnp.where(
        positions < block_count[..., None], block_values, jnp.zeros_like(block_values)
    )[0]
    tile_count = masked.shape[1]
    slot_count = masked.shape[2]
    weighted_rows = weighted.T
    picked = jnp.take(weighted_rows, block_sample.reshape(-1), axis=0)
    picked = picked.reshape(device_count, tile_count, slot_count, rank_width)
    values_in, rows_in = (
        lax.all_to_all(
            masked.reshape(device_count, -1), "row", split_axis=0, concat_axis=0, tiled=True
        ),
        lax.all_to_all(
            picked.reshape(device_count, -1), "row", split_axis=0, concat_axis=0, tiled=True
        ),
    )
    gathered = jnp.einsum(
        "stcr,stck->ktr",
        values_in.reshape(masked.shape),
        rows_in.reshape(picked.shape),
        preferred_element_type=jnp.float32,
    ).reshape(rank_width, -1)
    total_rows = gathered.shape[1] * device_count
    total_samples = sketch.shape[1] * device_count
    ridge = 0.05 * live_total / total_rows
    system = gram_matrix / total_samples + ridge * jnp.eye(rank_width, dtype=jnp.float32)
    lower_factor = jnp.linalg.cholesky(system)
    half_solved = lax.linalg.triangular_solve(lower_factor, gathered, left_side=True, lower=True)
    update = lax.linalg.triangular_solve(
        lower_factor, half_solved, left_side=True, lower=True, transpose_a=True
    )
    column_sums = lax.psum(jnp.sum(update * update, axis=1), "row")
    scales = jnp.sqrt(column_sums / total_rows + 1e-06)
    return ((update / scales[:, None]).astype(jnp.bfloat16), scales)


def solution(mesh):
    in_specs = (
        P(None, ("groups", "row")),
        P(None, ("groups", "row")),
        P(("groups", "row")),
        P(None, ("groups", "row"), None),
        P(("groups", "row")),
        P(("groups", "row"), None, None, None, None),
        P(("groups", "row"), None, None, None),
        P(("groups", "row"), None, None, None),
    )
    out_specs = (P(None, ("groups", "row")), P("groups"))
    return jax.shard_map(shards, mesh=mesh, in_specs=in_specs, out_specs=out_specs, check_vma=False)
```

profile of v0, /device:TPU:0, one launch (start us, length us, event | category | flops | bytes accessed | tf_op | source)
XLA Modules:
  0.0 222.8 jit_solution(864086933986388068)
XLA Ops:
  0.6 0.8 copy.44
  1.4 1.0 fusion.4
  2.4 0.5 broadcast.153
  3.0 1.0 reduce.8
  4.0 0.7 reshape.158
  4.6 7.4 %all-to-all-start.2 = ((bf16[16,2,1024]{2,1,0:T(2,128)(2,1)}), bf16[16,2,1024]{2,1,0:T(2,128)(2,1)S(1)}, u32[]{:S(2)}, u32[]{:S(2)}) async-start(bf16[16,2,1024]{2,1,0:T(2,128)(2,1)} %reshape.158), calls=%async_computation.2 | async-start | bytes 131072 | tf_op jit(solution)/shard_map/all_to_all | solution.py:34
  12.0 0.8 broadcast_subtract_fusion
  12.8 1.5 copy.37
  14.4 29.2 %gather_fusion.2 = bf16[8192,64]{1,0:T(8,128)(2,1)} fusion(bf16[64,4096]{0,1:T(8,128)(2,1)S(1)} %copy.37, s32[8192]{0:T(1024)S(1)} %fusion.12), kind=kCustom, calls=%fused_computation.1.clone | custom fusion | bytes 2129920 | tf_op jit(solution)/shard_map/jit(_take)/gather | solution.py:15
  43.6 5.8 %broadcast_select_fusion = bf16[8192,64]{1,0:T(8,128)(2,1)S(1)} fusion(bf16[8192,64]{1,0:T(8,128)(2,1)} %gather_fusion.2, pred[8192]{0:T(1024)(128)(4,1)S(1)} %compare_and_fusion), kind=kLoop, calls=%fused_computation.6 | loop fusion | flops 524288 | bytes 2105344 | tf_op jit(solution)/shard_map/jit(_take)/select_n | solution.py:15
  49.4 1.6 copy.38
  51.1 6.2 %all-to-all-start = ((bf16[64,16,512]{2,0,1:T(8,128)(2,1)}), bf16[64,16,512]{2,0,1:T(8,128)(2,1)}, u32[]{:S(2)}, u32[]{:S(2)}) async-start(bf16[64,16,512]{2,0,1:T(8,128)(2,1)} %copy.38), calls=%async_computation | async-start | bytes 2097152 | tf_op jit(solution)/shard_map/all_to_all | solution.py:16
  57.3 0.5 copy.36
  58.4 24.0 %gather_fusion.1 = bf16[8192,64]{1,0:T(8,128)(2,1)S(1)} fusion(bf16[64,4096]{0,1:T(8,128)(2,1)S(1)} %copy.36, s32[8192]{0:T(1024)S(1)} %fusion.13), kind=kCustom, calls=%fused_computation.clone | custom fusion | bytes 2129920 | tf_op jit(solution)/shard_map/jit(_take)/gather | solution.py:13
  82.5 0.6 convert_reduce_fusion
  83.1 0.4 reduce.7
  83.6 3.3 %copy.39 = f32[64,16,512]{0,2,1:T(8,128)} copy(bf16[64,16,512]{2,0,1:T(8,128)(2,1)} %all-to-all-done) | data formatting | bytes 3145728 | tf_op jit(solution)/shard_map/convert_element_type | solution.py:19
  86.9 9.6 %fusion = (bf16[8192,64]{1,0:T(8,128)(2,1)}, f32[64,8192]{0,1:T(8,128)S(1)}) fusion(f32[8192]{0:T(1024)S(1)} %copy-done.2, f32[64,16,512]{0,2,1:T(8,128)} %copy.39, bf16[8192,64]{1,0:T(8,128)(2,1)S(1)} %gather_fusion.1, pred[8192]{0:T(1024)(128)(4,1)S(1)} %compare_and_fusion.1), kind=kLoop, calls=%fused_computation.5 | loop fusion | flops 3145728 | bytes 6332416 | tf_op jit(solution)/shard_map/transpose | solution.py:30
  96.5 7.0 %fusion.14 = f32[64,64]{1,0:T(8,128)S(1)} fusion(f32[64,8192]{0,1:T(8,128)S(1)} %get-tuple-element.6), kind=kOutput, calls=%fused_computation.43 | convolution fusion | flops 402653184 | bytes 2113536 | tf_op jit(solution)/shard_map/dot_general | solution.py:20
  103.5 63.0 %all-reduce = (f32[64,64]{1,0:T(8,128)S(1)}, f32[]{:T(128)}) all-reduce(f32[64,64]{1,0:T(8,128)S(1)} %fusion.14, f32[]{:T(128)} %convert_reduce_fusion), channel_id=1, replica_groups=mesh['groups'=2,'row'=16] {'row'}, use_global_device_ids=true, to_apply=%region_0.0 | all-reduce | flops 4097 | bytes 32776 | tf_op jit(solution)/shard_map/psum | solution.py:22
  167.2 5.8 %cholesky.16 = f32[64,64]{1,0:T(8,128)S(1)} custom-call(f32[64,64]{1,0:T(8,128)S(1)} %fusion.11), custom_call_target="Cholesky" | custom-call | tf_op jit(solution)/shard_map/jit(cholesky)/cholesky | solution.py:51
  173.1 0.7 compare_reduce_fusion
  173.8 2.6 %gather_fusion = bf16[256,64]{1,0:T(8,128)(2,1)S(1)} fusion(bf16[8192,64]{1,0:T(8,128)(2,1)} %get-tuple-element.5, s32[1024]{0:T(1024)S(1)} %pad_clamp_fusion), kind=kCustom, calls=%fused_computation.2 | custom fusion | bytes 66560 | tf_op jit(solution)/shard_map/jit(_take)/gather | solution.py:31
  176.6 0.7 reduce.9
  177.2 0.6 reshape.160
  177.9 3.5 %all-to-all-start.1 = ((bf16[16,2,512]{2,1,0:T(2,128)(2,1)}), bf16[16,2,512]{2,1,0:T(2,128)(2,1)S(1)}, u32[]{:S(2)}, u32[]{:S(2)}) async-start(bf16[16,2,512]{2,1,0:T(2,128)(2,1)} %reshape.160), calls=%async_computation.1 | async-start | bytes 65536 | tf_op jit(solution)/shard_map/all_to_all | solution.py:37
  181.4 0.7 fusion.7
  182.1 4.9 %custom-call.8 = f32[1,64,64]{1,2,0:T(8,128)S(1)} custom-call(f32[1,64,64]{2,1,0:T(8,128)S(1)} %fusion.7), custom_call_target="InvertDiagBlocksLowerTriangular" | custom-call | tf_op jit(solution)/shard_map/triangular_solve | solution.py:53
  187.0 1.0 all-to-all-done.1
  188.8 0.4 multiply_reduce_fusion
  189.2 32.8 %psum.23 = f32[64]{0:T(128)S(1)} all-reduce(f32[64]{0:T(128)S(1)} %get-tuple-element.7), channel_id=1, replica_groups=mesh['groups'=2,'row'=16] {'row'}, use_global_device_ids=true, to_apply=%region_6.8 | all-reduce | flops 64 | bytes 512 | tf_op jit(solution)/shard_map/psum | solution.py:56
  222.0 0.7 divide_convert_fusion
  (41 shorter events, 1.9 us)
Async XLA Ops:
  4.6 46.5 %all-to-all-start.2 = ((bf16[16,2,1024]{2,1,0:T(2,128)(2,1)}), bf16[16,2,1024]{2,1,0:T(2,128)(2,1)S(1)}, u32[]{:S(2)}, u32[]{:S(2)}) async-start(bf16[16,2,1024]{2,1,0:T(2,128)(2,1)} %reshape.158), calls=%async_computation.2 | async-start | bytes 131072 | tf_op jit(solution)/shard_map/all_to_all | solution.py:34
  49.4 7.9 %copy-start = (bf16[64,4096]{1,0:T(8,128)(2,1)S(1)}, bf16[64,4096]{1,0:T(8,128)(2,1)}, u32[]{:S(2)}) copy-start(bf16[64,4096]{1,0:T(8,128)(2,1)} %param.10) | copy-start | bytes 1572868
  51.1 6.7 %copy-start.3 = (s32[1,16,4,4]{1,3,2,0:T(4,128)S(1)}, s32[1,16,4,4]{1,3,2,0:T(4,128)}, u32[]{:S(2)}) copy-start(s32[1,16,4,4]{1,3,2,0:T(4,128)} %param.16) | copy-start | bytes 3076
  51.1 7.3 %copy-start.1 = (s32[8192]{0:T(1024)S(1)}, s32[8192]{0:T(1024)}, u32[]{:S(2)}) copy-start(s32[8192]{0:T(1024)} %param.12) | copy-start | bytes 98308
  51.1 32.5 %all-to-all-start = ((bf16[64,16,512]{2,0,1:T(8,128)(2,1)}), bf16[64,16,512]{2,0,1:T(8,128)(2,1)}, u32[]{:S(2)}, u32[]{:S(2)}) async-start(bf16[64,16,512]{2,0,1:T(8,128)(2,1)} %copy.38), calls=%async_computation | async-start | bytes 2097152 | tf_op jit(solution)/shard_map/all_to_all | solution.py:16
  58.4 24.1 %copy-start.4 = (s32[1,16,4,4]{1,3,2,0:T(4,128)S(1)}, s32[1,16,4,4]{1,3,2,0:T(4,128)}, u32[]{:S(2)}) copy-start(s32[1,16,4,4]{1,3,2,0:T(4,128)} %param.17) | copy-start | bytes 3076
  83.5 3.3 %copy-start.2 = (f32[8192]{0:T(1024)S(1)}, f32[8192]{0:T(1024)}, u32[]{:S(2)}) copy-start(f32[8192]{0:T(1024)} %param.14) | copy-start | bytes 98308
  177.9 10.1 %all-to-all-start.1 = ((bf16[16,2,512]{2,1,0:T(2,128)(2,1)}), bf16[16,2,512]{2,1,0:T(2,128)(2,1)S(1)}, u32[]{:S(2)}, u32[]{:S(2)}) async-start(bf16[16,2,512]{2,1,0:T(2,128)(2,1)} %reshape.160), calls=%async_computation.1 | async-start | bytes 65536 | tf_op jit(solution)/shard_map/all_to_all | solution.py:37
  222.0 0.7 copy-start.5
where the time goes:
time: 224 us; the launch traced here: 223 us
  blocking collectives  95.8 us (43%)
  local copies, waits for them, and re-layouts  66.4 us (30%)
  other arithmetic  33 us (15%)
  starting transfers between devices  17.1 us (8%)
  matrix products  7.89 us (4%)
    psum x1, blocking collectives, shards(): gram_matrix, live_total = lax.psum((gram_local, live_local), 'row')  63 us
    psum x1, blocking collectives, shards(): column_sums = lax.psum(jnp.sum(update * update, axis=1), 'row')  32.8 us
    gather x1, local copies, waits for them, and re-layouts, shards(): jnp.take(factor_c, c_local, axis=1).reshape(rank_width, device_count, -1)  29.2 us
    gather x1, local copies, waits for them, and re-layouts, shards(): jnp.take(factor_b, sample_j - device_index * factor_b.shape[1], axis=1)  24 us
    transpose x1, other arithmetic, shards(): weighted_rows = weighted.T  9.6 us
    all_to_all x1, starting transfers between devices, shards(): lax.all_to_all(masked.reshape(device_count, -1), 'row', split_axis=0, con...  7.41 us
    dot_general x1, matrix products, shards(): gram_local = jnp.dot(sketch, sketch.T, precision=lax.Precision.HIGHEST)  6.99 us
    another operation x3, other arithmetic, shards(): lower_factor = jnp.linalg.cholesky(system)  6.6 us
  transfers between devices with their start and end apart: 3, of which 1 were waited for; matrix products, arithmetic and copies ran while one was open for 32% of the time, Pallas kernels for 0%

commit v1 on v0

v1 whole, which is shorter than its diff:
```python
import functools

import jax
import jax.numpy as jnp
from jax import lax
from jax.experimental import pallas as pl
from jax.experimental.pallas import tpu as pltpu
from jax.sharding import PartitionSpec as P

NT = (((1,), (1,)), ((), ()))
TN = (((0,), (0,)), ((), ()))
MESH = pl.DeviceIdType.MESH


def fold_table(table_ref, folded, width):
    rank = table_ref.shape[0]
    for part in range(table_ref.shape[1] // width):
        folded[part * rank : (part + 1) * rank, :] = table_ref[
            :, part * width : (part + 1) * width
        ]


def pick_columns(folded, index, rank):
    width = folded.shape[1]
    count = index.shape[1]
    low = lax.rem(index, width)
    high = lax.div(index, width)
    rows = lax.broadcasted_iota(jnp.int16, (width, count), 0)
    one_hot = jnp.where(rows == low.astype(jnp.int16), jnp.bfloat16(1), jnp.bfloat16(0))
    products = jnp.dot(folded[...], one_hot, preferred_element_type=jnp.float32)
    picked = products[:rank]
    high = jnp.broadcast_to(high, (rank, count))
    for part in range(1, folded.shape[0] // rank):
        picked = jnp.where(high == part, products[part * rank : (part + 1) * rank], picked)
    return picked


def inverse(matrix):
    order = matrix.shape[0]
    lanes = lax.broadcasted_iota(jnp.int32, (1, order), 1)
    rows = lax.broadcasted_iota(jnp.int32, (order, 1), 0)
    for k in range(order):
        row = matrix[k : k + 1, :]
        column = matrix[:, k : k + 1]
        pivot = 1.0 / row[:, k : k + 1]
        scaled = jnp.where(lanes == k, 1.0, row) * pivot
        matrix = jnp.where(
            rows == k, scaled, jnp.where(lanes == k, 0.0, matrix) - column * scaled
        )
    return matrix


def kernel(
    n,
    tiles,
    slots,
    width,
    total_rows,
    total_samples,
    b_ref,
    c_ref,
    j_ref,
    k_ref,
    w_ref,
    values_ref,
    sample_ref,
    count_ref,
    out_ref,
    scales_ref,
    folded_b,
    folded_c,
    c_out,
    c_in,
    b_weighted,
    values_out,
    values_in,
    picks_out,
    picks_in,
    gram_out,
    gram_in,
    sums_out,
    sums_in,
    c_send,
    c_recv,
    values_send,
    values_recv,
    picks_send,
    picks_recv,
    gram_send,
    gram_recv,
    sums_send,
    sums_recv,
):
    me = lax.axis_index("row")
    rank, b_rows = b_ref.shape
    c_rows = c_ref.shape[1]
    half = rank // 2
    per_peer = tiles * slots
    blocks = n * per_peer
    chunk = c_in.shape[2]

    def each_peer(body):
        def step(offset, carry):
            body(lax.rem(me + offset, n))
            return carry

        lax.fori_loop(1, n, step, 0)

    def copy_to(peer, source, target, send, recv):
        return pltpu.make_async_remote_copy(
            src_ref=source,
            dst_ref=target.at[me],
            send_sem=send.at[peer],
            recv_sem=recv.at[me],
            device_id={"row": peer},
            device_id_type=MESH,
        )

    def copy_from(peer, source, target, send, recv):
        return pltpu.make_async_remote_copy(
            src_ref=source,
            dst_ref=target.at[peer],
            send_sem=send.at[peer],
            recv_sem=recv.at[peer],
            device_id={"row": peer},
            device_id_type=MESH,
        )

    barrier = pltpu.get_barrier_semaphore()
    each_peer(
        lambda peer: pl.semaphore_signal(
            barrier, inc=1, device_id={"row": peer}, device_id_type=MESH
        )
    )
    fold_table(c_ref, folded_c, width)
    fold_table(b_ref, folded_b, width)
    lanes = lax.broadcasted_iota(jnp.int32, (blocks, 128), 1)
    live = lanes < count_ref[...]
    masked = jnp.where(live, values_ref[...].astype(jnp.float32), 0.0).astype(jnp.bfloat16)
    values_out[...] = masked.reshape(values_out.shape)
    values_in[me] = values_out[me]
    c_in[me] = pick_columns(folded_c, k_ref[me] - me * c_rows, rank).astype(jnp.bfloat16)
    pl.semaphore_wait(barrier, n - 1)

    def send_c(peer):
        c_out[peer] = pick_columns(folded_c, k_ref[peer] - me * c_rows, rank).astype(
            jnp.bfloat16
        )
        copy_to(peer, c_out.at[peer], c_in, c_send, c_recv).start()

    each_peer(send_c)
    each_peer(
        lambda peer: copy_to(
            peer, values_out.at[peer], values_in, values_send, values_recv
        ).start()
    )

    def pick_b(part, carry):
        picked = pick_columns(folded_b, j_ref[part] - me * b_rows, rank)
        b_weighted[part] = w_ref[part] * picked
        return carry

    lax.fori_loop(0, n, pick_b, 0)

    columns = lax.broadcasted_iota(jnp.int32, (blocks, chunk), 1)

    def add_chunk(part, carry):
        gram, picks = carry
        weights = w_ref[part]
        sketch = b_weighted[part] * c_in[part].astype(jnp.float32)
        top = sketch.astype(jnp.bfloat16)
        rest = (sketch - top.astype(jnp.float32)).astype(jnp.bfloat16)
        both = jnp.concatenate([top, rest], axis=0)
        gram = gram + lax.dot_general(both, both, NT, preferred_element_type=jnp.float32)
        weighted = (weights * sketch).astype(jnp.bfloat16)
        chosen = columns == sample_ref[...] - part * chunk
        chosen = jnp.where(chosen, 1.0, 0.0).astype(jnp.bfloat16)
        picks = picks + lax.dot_general(
            chosen, weighted, NT, preferred_element_type=jnp.float32
        )
        return gram, picks

    def add_peer(offset, carry):
        part = lax.rem(me + n - offset, n)
        copy_from(part, c_out.at[part], c_in, c_send, c_recv).wait_recv()
        return add_chunk(part, carry)

    carry = (
        jnp.zeros((2 * rank, 2 * rank), jnp.float32),
        jnp.zeros((blocks, rank), jnp.float32),
    )
    carry = add_chunk(me, carry)
    gram, picks = lax.fori_loop(1, n, add_peer, carry)

    gram = gram[:rank, :rank] + gram[:rank, rank:] + gram[rank:, :rank] + gram[rank:, rank:]
    live_local = jnp.sum(count_ref[...].astype(jnp.float32), axis=0, keepdims=True)
    gram_out[:half, :] = jnp.concatenate([gram[:half], gram[half:]], axis=1)
    gram_out[half:, :] = jnp.broadcast_to(live_local, (8, 2 * rank))
    gram_in[me] = gram_out[...]
    picks = jnp.concatenate([picks, jnp.zeros_like(picks)], axis=1).astype(jnp.bfloat16)
    picks_out[...] = picks.reshape(picks_out.shape)
    picks_in[me] = picks_out[me]

    def send_sums(peer):
        copy_to(peer, gram_out, gram_in, gram_send, gram_recv).start()
        copy_to(peer, picks_out.at[peer], picks_in, picks_send, picks_recv).start()

    each_peer(send_sums)

    def receive_sums(peer):
        copy_from(peer, gram_out, gram_in, gram_send, gram_recv).wait_recv()

    each_peer(receive_sums)
    total = lax.fori_loop(
        1, n, lambda part, carry: carry + gram_in[part], gram_in[0]
    )
    ridge = 0.05 * total[half : half + 1, :rank] / total_rows
    gram = jnp.concatenate([total[:half, :rank], total[:half, rank:]], axis=0)
    gram_rows = lax.broadcasted_iota(jnp.int32, (rank, rank), 0)
    diagonal = gram_rows == lax.broadcasted_iota(jnp.int32, (rank, rank), 1)
    system = gram / total_samples + jnp.where(diagonal, ridge, 0.0)
    inverted = inverse(system)

    def receive_blocks(peer):
        copy_from(
            peer, values_out.at[peer], values_in, values_send, values_recv
        ).wait_recv()
        copy_from(peer, picks_out.at[peer], picks_in, picks_send, picks_recv).wait_recv()

    each_peer(receive_blocks)
    arrived = values_in[...].reshape(blocks, 128).astype(jnp.float32)
    block_rows = lax.broadcasted_iota(jnp.int32, (blocks, 128), 0)
    tile_of = lax.rem(lax.div(block_rows, slots), tiles)
    spread = jnp.concatenate(
        [jnp.where(tile_of == tile, arrived, 0.0) for tile in range(tiles)], axis=1
    ).astype(jnp.bfloat16)
    gathered = lax.dot_general(
        picks_in[...].reshape(blocks, 2 * rank), spread, TN, preferred_element_type=jnp.float32
    )[:rank]
    update = jnp.dot(
        inverted,
        gathered,
        precision=lax.Precision.HIGHEST,
        preferred_element_type=jnp.float32,
    )
    squares = jnp.sum(update * update, axis=1, keepdims=True)
    squares = jnp.sum(jnp.where(diagonal, squares, 0.0), axis=0, keepdims=True)
    squares = jnp.concatenate([squares, jnp.zeros_like(squares)], axis=1)
    sums_out[...] = jnp.broadcast_to(squares, sums_out.shape)
    sums_in[me] = sums_out[...]
    each_peer(
        lambda peer: copy_to(peer, sums_out, sums_in, sums_send, sums_recv).start()
    )
    each_peer(
        lambda peer: copy_from(peer, sums_out, sums_in, sums_send, sums_recv).wait_recv()
    )
    sums = lax.fori_loop(1, n, lambda part, carry: carry + sums_in[part], sums_in[0])
    scales = jnp.sqrt(sums[:1, :rank] / total_rows + 1e-06)
    scales_ref[...] = scales
    scale_column = jnp.sum(jnp.where(diagonal, scales, 0.0), axis=1, keepdims=True)
    out_ref[...] = (update / scale_column).astype(out_ref.dtype)

    def finish(peer):
        copy_to(peer, c_out.at[peer], c_in, c_send, c_recv).wait_send()
        copy_to(peer, values_out.at[peer], values_in, values_send, values_recv).wait_send()
        copy_to(peer, gram_out, gram_in, gram_send, gram_recv).wait_send()
        copy_to(peer, picks_out.at[peer], picks_in, picks_send, picks_recv).wait_send()
        copy_to(peer, sums_out, sums_in, sums_send, sums_recv).wait_send()

    each_peer(finish)


def shards(
    factor_b, factor_c, sample_j, sample_k, sample_weight, block_values, block_sample, block_count
):
    rank, b_rows = factor_b.shape
    n, _, chunk = sample_k.shape
    _, _, tiles, slots, tile_rows = block_values.shape
    samples = sample_j.shape[0]
    per_peer = tiles * slots
    blocks = n * per_peer
    width = 512
    bf16, f32 = jnp.bfloat16, jnp.float32
    vmem = pl.BlockSpec(memory_space=pltpu.VMEM)
    factor_new, scales = pl.pallas_call(
        functools.partial(
            kernel, n, tiles, slots, width, tiles * tile_rows * n, samples * n
        ),
        out_shape=(
            jax.ShapeDtypeStruct((rank, tiles * tile_rows), bf16),
            jax.ShapeDtypeStruct((1, rank), f32),
        ),
        in_specs=[vmem] * 8,
        out_specs=(vmem, vmem),
        scratch_shapes=[
            pltpu.VMEM((b_rows // width * rank, width), bf16),
            pltpu.VMEM((factor_c.shape[1] // width * rank, width), bf16),
            pltpu.VMEM((n, rank, chunk), bf16),
            pltpu.VMEM((n, rank, chunk), bf16),
            pltpu.VMEM((n, rank, chunk), f32),
            pltpu.VMEM((n, per_peer, tile_rows), bf16),
            pltpu.VMEM((n, per_peer, tile_rows), bf16),
            pltpu.VMEM((n, per_peer, 2 * rank), bf16),
            pltpu.VMEM((n, per_peer, 2 * rank), bf16),
            pltpu.VMEM((rank // 2 + 8, 2 * rank), f32),
            pltpu.VMEM((n, rank // 2 + 8, 2 * rank), f32),
            pltpu.VMEM((8, 2 * rank), f32),
            pltpu.VMEM((n, 8, 2 * rank), f32),
        ]
        + [pltpu.SemaphoreType.DMA((n,))] * 10,
        compiler_params=pltpu.CompilerParams(collective_id=0, has_side_effects=True),
    )(
        factor_b,
        factor_c,
        sample_j.reshape(n, 1, chunk),
        sample_k,
        sample_weight.reshape(n, 1, chunk),
        block_values.reshape(blocks, tile_rows),
        block_sample.reshape(blocks, 1),
        block_count.reshape(blocks, 1),
    )
    return factor_new, scales.reshape(rank)


def solution(mesh):
    in_specs = (
        P(None, ("groups", "row")),
        P(None, ("groups", "row")),
        P(("groups", "row")),
        P(None, ("groups", "row"), None),
        P(("groups", "row")),
        P(("groups", "row"), None, None, None, None),
        P(("groups", "row"), None, None, None),
        P(("groups", "row"), None, None, None),
    )
    out_specs = (P(None, ("groups", "row")), P("groups"))
    return jax.shard_map(shards, mesh=mesh, in_specs=in_specs, out_specs=out_specs, check_vma=False)
```

time: 224 us -> 66 us (0.29)
  blocking collectives: 95.8 us -> 0 us
  local copies, waits for them, and re-layouts: 66.4 us -> 4.4 us
  Pallas kernels: 0 us -> 60.8 us
  other arithmetic: 33 us -> 0 us
  starting transfers between devices: 17.1 us -> 0 us
  matrix products: 7.89 us -> 0 us
    psum x2 -> x0, blocking collectives: 95.8 us -> none  [the longest x1 63 us: shards(): gram_matrix, live_total = lax.psum((gram_local, live_local), 'row')]
    pallas_call x0 -> x1, Pallas kernels: none -> 60.8 us  [shards(): pl.pallas_call(functools.partial(kernel, n, tiles, slots, width, tiles *...]
    gather x4 -> x0, local copies, waits for them, and re-layouts: 56 us -> none  [the longest x1 29.2 us: shards(): jnp.take(factor_c, c_local, axis=1).reshape(rank_width, device_count, -1)]
    all_to_all x3 -> x0, starting transfers between devices: 17.1 us -> none  [the longest x1 7.41 us: shards(): lax.all_to_all(masked.reshape(device_count, -1), 'row', split_axis=0, con...]
    another operation x5 -> x0, other arithmetic: 12.2 us -> none  [the longest x3 6.6 us: shards(): lower_factor = jnp.linalg.cholesky(system)]
    transpose x1 -> x0, other arithmetic: 9.6 us -> none  [shards(): weighted_rows = weighted.T]
    select_n x5 -> x0, other arithmetic: 7.46 us -> none  [the longest x1 5.82 us: shards(): jnp.take(factor_c, c_local, axis=1).reshape(rank_width, device_count, -1)]
    dot_general x2 -> x0, matrix products: 7.2 us -> none  [the longest x1 6.99 us: shards(): gram_local = jnp.dot(sketch, sketch.T, precision=lax.Precision.HIGHEST)]
  transfers between devices with their start and end apart: 3 -> 0, of which waited for: 1 -> 0; matrix products, arithmetic and copies ran while one was open for 32% -> 0% of each run, Pallas kernels for 0% -> 0%
where the time goes in v1:
time: 66 us; the launch traced here: 65.8 us
  Pallas kernels  60.8 us (92%)
  local copies, waits for them, and re-layouts  4.4 us (7%)
  between operations  0.66 us (1%)
    pallas_call x1, Pallas kernels, shards(): pl.pallas_call(functools.partial(kernel, n, tiles, slots, width, tiles *...  60.8 us
    unnamed x8, local copies, waits for them, and re-layouts  2.9 us

profile of v1, /device:TPU:0, one launch (start us, length us, event | category | flops | bytes accessed | tf_op | source)
XLA Modules:
  0.0 65.8 jit_solution(9681376377183481503)
XLA Ops:
  0.6 0.0 copy-start
  0.6 0.8 %copy.12 = s32[1,16,4,4]{3,2,1,0:T(4,128)S(1)} copy(s32[1,16,4,4]{1,3,2,0:T(4,128)} %param.14) | data formatting | bytes 2048 | tf_op args[6]
  1.4 0.0 copy-done
  1.4 0.1 copy.13
  1.6 0.7 %reshape.29.count_ref = s32[256,1]{1,0:T(8,128)} reshape(s32[1,16,4,4]{3,2,1,0:T(4,128)S(1)} %copy.13) | data formatting | bytes 2048 | tf_op jit(solution)/shard_map/reshape | solution.py:320
  2.3 0.7 %reshape.28.sample_ref = s32[256,1]{1,0:T(8,128)} reshape(s32[1,16,4,4]{3,2,1,0:T(4,128)S(1)} %copy.12) | data formatting | bytes 2048 | tf_op jit(solution)/shard_map/reshape | solution.py:319
  3.0 60.8 %shard_map.95 = (bf16[64,512]{1,0:T(8,128)(2,1)}, f32[1,64]{1,0:T(1,128)}) custom-call(bf16[64,4096]{1,0:T(8,128)(2,1)} %b_ref.1, bf16[64,4096]{1,0:T(8,128)(2,1)} %c_ref.1, s32[16,1,512]{2,1,0:T(1,128)} %bitcast.5, s32[16,1,512]{2,1,0:T(1,128)} %k_ref.1, f32[16,1,512]{2,1,0:T(1,128)} %bitcast.6, bf16[256,128]{1,0:T(8,128)(2,1)} %bitcast.4, ...), custom_call_target="tpu_custom_call" | custom-call | tf_op jit(solution)/shard_map/pallas_call | solution.py:285
  63.8 0.0 copy-start.1
  63.8 1.5 %copy.18 = bf16[64,512]{1,0:T(8,128)(2,1)} copy(bf16[64,512]{1,0:T(8,128)(2,1)} %get-tuple-element.8) | data formatting | bytes 131072
  65.3 0.0 copy-done.1
  65.3 0.5 copy.19
Async XLA Ops:
  0.6 0.8 %copy-start = (s32[1,16,4,4]{1,3,2,0:T(4,128)S(1)}, s32[1,16,4,4]{1,3,2,0:T(4,128)}, u32[]{:S(2)}) copy-start(s32[1,16,4,4]{1,3,2,0:T(4,128)} %param.15) | copy-start | bytes 3076
  63.8 1.5 %copy-start.1 = (f32[1,64]{1,0:T(1,128)S(1)}, f32[1,64]{1,0:T(1,128)}, u32[]{:S(2)}) copy-start(f32[1,64]{1,0:T(1,128)} %get-tuple-element.5) | copy-start | bytes 772

commit v2 on v1

--- a/solution.py
+++ b/solution.py
@@ -33,6 +33,21 @@
     for part in range(1, folded.shape[0] // rank):
         picked = jnp.where(high == part, products[part * rank : (part + 1) * rank], picked)
     return picked
+
+
+def partner(me, mask, n):
+    other, bit = 0, 1
+    while bit < n:
+        other = other + bit * lax.rem(lax.div(me, bit) + lax.div(mask, bit), 2)
+        bit *= 2
+    return other
+
+
+def block_column(table_ref):
+    table = jnp.concatenate([table_ref[tile] for tile in range(table_ref.shape[0])], axis=0)
+    return jnp.concatenate(
+        [table[:, peer : peer + 1] for peer in range(table.shape[1])], axis=0
+    )
 
 
 def inverse(matrix):
@@ -78,6 +93,9 @@
     picks_in,
     gram_out,
     gram_in,
+    share_out,
+    share_in,
+    sample_column,
     sums_out,
     sums_in,
     c_send,
@@ -88,20 +106,22 @@
     picks_recv,
     gram_send,
     gram_recv,
+    share_send,
+    share_recv,
     sums_send,
     sums_recv,
 ):
     me = lax.axis_index("row")
     rank, b_rows = b_ref.shape
     c_rows = c_ref.shape[1]
-    half = rank // 2
+    share = rank // n
     per_peer = tiles * slots
     blocks = n * per_peer
     chunk = c_in.shape[2]
 
     def each_peer(body):
-        def step(offset, carry):
-            body(lax.rem(me + offset, n))
+        def step(turn, carry):
+            body(partner(me, n - turn, n))
             return carry
 
         lax.fori_loop(1, n, step, 0)
@@ -135,7 +155,8 @@
     fold_table(c_ref, folded_c, width)
     fold_table(b_ref, folded_b, width)
     lanes = lax.broadcasted_iota(jnp.int32, (blocks, 128), 1)
-    live = lanes < count_ref[...]
+    counts = block_column(count_ref)
+    live = lanes < counts
     masked = jnp.where(live, values_ref[...].astype(jnp.float32), 0.0).astype(jnp.bfloat16)
     values_out[...] = masked.reshape(values_out.shape)
     values_in[me] = values_out[me]
@@ -163,6 +184,8 @@
     lax.fori_loop(0, n, pick_b, 0)
 
     columns = lax.broadcasted_iota(jnp.int32, (blocks, chunk), 1)
+    sample_column[...] = block_column(sample_ref)
+    counts = block_column(count_ref)
 
     def add_chunk(part, carry):
         gram, picks = carry
@@ -173,15 +196,15 @@
         both = jnp.concatenate([top, rest], axis=0)
         gram = gram + lax.dot_general(both, both, NT, preferred_element_type=jnp.float32)
         weighted = (weights * sketch).astype(jnp.bfloat16)
-        chosen = columns == sample_ref[...] - part * chunk
+        chosen = columns == sample_column[...] - part * chunk
         chosen = jnp.where(chosen, 1.0, 0.0).astype(jnp.bfloat16)
         picks = picks + lax.dot_general(
             chosen, weighted, NT, preferred_element_type=jnp.float32
         )
         return gram, picks
 
-    def add_peer(offset, carry):
-        part = lax.rem(me + n - offset, n)
+    def add_peer(turn, carry):
+        part = partner(me, n - turn, n)
         copy_from(part, c_out.at[part], c_in, c_send, c_recv).wait_recv()
         return add_chunk(part, carry)
 
@@ -193,33 +216,33 @@
     gram, picks = lax.fori_loop(1, n, add_peer, carry)
 
     gram = gram[:rank, :rank] + gram[:rank, rank:] + gram[rank:, :rank] + gram[rank:, rank:]
-    live_local = jnp.sum(count_ref[...].astype(jnp.float32), axis=0, keepdims=True)
-    gram_out[:half, :] = jnp.concatenate([gram[:half], gram[half:]], axis=1)
-    gram_out[half:, :] = jnp.broadcast_to(live_local, (8, 2 * rank))
-    gram_in[me] = gram_out[...]
+    live_local = jnp.sum(counts.astype(jnp.float32), axis=0, keepdims=True)
+    gram = jnp.concatenate([gram, jnp.broadcast_to(live_local, gram.shape)], axis=1)
+    gram_out[...] = jnp.zeros_like(gram_out)
+    for part in range(n):
+        gram_out[part, :share, :] = gram[part * share : (part + 1) * share]
+    gram_in[me] = gram_out[me]
     picks = jnp.concatenate([picks, jnp.zeros_like(picks)], axis=1).astype(jnp.bfloat16)
     picks_out[...] = picks.reshape(picks_out.shape)
     picks_in[me] = picks_out[me]
 
     def send_sums(peer):
-        copy_to(peer, gram_out, gram_in, gram_send, gram_recv).start()
+        copy_to(peer, gram_out.at[peer], gram_in, gram_send, gram_recv).start()
         copy_to(peer, picks_out.at[peer], picks_in, picks_send, picks_recv).start()
 
     each_peer(send_sums)
 
     def receive_sums(peer):
-        copy_from(peer, gram_out, gram_in, gram_send, gram_recv).wait_recv()
+        copy_from(peer, gram_out.at[peer], gram_in, gram_send, gram_recv).wait_recv()
 
     each_peer(receive_sums)
-    total = lax.fori_loop(
+    share_out[...] = lax.fori_loop(
         1, n, lambda part, carry: carry + gram_in[part], gram_in[0]
     )
-    ridge = 0.05 * total[half : half + 1, :rank] / total_rows
-    gram = jnp.concatenate([total[:half, :rank], total[:half, rank:]], axis=0)
-    gram_rows = lax.broadcasted_iota(jnp.int32, (rank, rank), 0)
-    diagonal = gram_rows == lax.broadcasted_iota(jnp.int32, (rank, rank), 1)
-    system = gram / total_samples + jnp.where(diagonal, ridge, 0.0)
-    inverted = inverse(system)
+    share_in[me] = share_out[...]
+    each_peer(
+        lambda peer: copy_to(peer, share_out, share_in, share_send, share_recv).start()
+    )
 
     def receive_blocks(peer):
         copy_from(
@@ -237,6 +260,15 @@
     gathered = lax.dot_general(
         picks_in[...].reshape(blocks, 2 * rank), spread, TN, preferred_element_type=jnp.float32
     )[:rank]
+    each_peer(
+        lambda peer: copy_from(peer, share_out, share_in, share_send, share_recv).wait_recv()
+    )
+    total = jnp.concatenate([share_in[part][:share] for part in range(n)], axis=0)
+    ridge = 0.05 * total[:1, rank:] / total_rows
+    gram_rows = lax.broadcasted_iota(jnp.int32, (rank, rank), 0)
+    diagonal = gram_rows == lax.broadcasted_iota(jnp.int32, (rank, rank), 1)
+    system = total[:, :rank] / total_samples + jnp.where(diagonal, ridge, 0.0)
+    inverted = inverse(system)
     update = jnp.dot(
         inverted,
         gathered,
@@ -263,7 +295,8 @@
     def finish(peer):
         copy_to(peer, c_out.at[peer], c_in, c_send, c_recv).wait_send()
         copy_to(peer, values_out.at[peer], values_in, values_send, values_recv).wait_send()
-        copy_to(peer, gram_out, gram_in, gram_send, gram_recv).wait_send()
+        copy_to(peer, gram_out.at[peer], gram_in, gram_send, gram_recv).wait_send()
+        copy_to(peer, share_out, share_in, share_send, share_recv).wait_send()
         copy_to(peer, picks_out.at[peer], picks_in, picks_send, picks_recv).wait_send()
         copy_to(peer, sums_out, sums_in, sums_send, sums_recv).wait_send()
 
@@ -302,12 +335,15 @@
             pltpu.VMEM((n, per_peer, tile_rows), bf16),
             pltpu.VMEM((n, per_peer, 2 * rank), bf16),
             pltpu.VMEM((n, per_peer, 2 * rank), bf16),
-            pltpu.VMEM((rank // 2 + 8, 2 * rank), f32),
-            pltpu.VMEM((n, rank // 2 + 8, 2 * rank), f32),
+            pltpu.VMEM((n, 8, 2 * rank), f32),
+            pltpu.VMEM((n, 8, 2 * rank), f32),
+            pltpu.VMEM((8, 2 * rank), f32),
+            pltpu.VMEM((n, 8, 2 * rank), f32),
+            pltpu.VMEM((blocks, 1), jnp.int32),
             pltpu.VMEM((8, 2 * rank), f32),
             pltpu.VMEM((n, 8, 2 * rank), f32),
         ]
-        + [pltpu.SemaphoreType.DMA((n,))] * 10,
+        + [pltpu.SemaphoreType.DMA((n,))] * 12,
         compiler_params=pltpu.CompilerParams(collective_id=0, has_side_effects=True),
     )(
         factor_b,
@@ -316,8 +352,8 @@
         sample_k,
         sample_weight.reshape(n, 1, chunk),
         block_values.reshape(blocks, tile_rows),
-        block_sample.reshape(blocks, 1),
-        block_count.reshape(blocks, 1),
+        block_sample[0].transpose(1, 2, 0),
+        block_count[0].transpose(1, 2, 0),
     )
     return factor_new, scales.reshape(rank)
 

time: 66 us -> 59.7 us (0.905)
  Pallas kernels: 60.8 us -> 56.9 us
  local copies, waits for them, and re-layouts: 4.4 us -> 1.99 us
    pallas_call x1, Pallas kernels: 60.8 us -> 56.9 us  [shards(): pl.pallas_call(functools.partial(kernel, n, tiles, slots, width, tiles *...]
    reshape x2 -> x0, local copies, waits for them, and re-layouts: 1.49 us -> none  [the longest x1 0.75 us: shards(): block_sample.reshape(blocks, 1)]
    unnamed x8 -> x4, local copies, waits for them, and re-layouts: 2.9 us -> 1.99 us
where the time goes in v2:
time: 59.7 us; the launch traced here: 59.5 us
  Pallas kernels  56.9 us (95%)
  local copies, waits for them, and re-layouts  1.99 us (3%)
  between operations  0.65 us (1%)
    pallas_call x1, Pallas kernels, shards(): pl.pallas_call(functools.partial(kernel, n, tiles, slots, width, tiles *...  56.9 us
    unnamed x4, local copies, waits for them, and re-layouts  1.99 us

profile of v2, /device:TPU:0, one launch (start us, length us, event | category | flops | bytes accessed | tf_op | source)
XLA Modules:
  0.0 59.5 jit_solution(15553964342946624761)
XLA Ops:
  0.6 56.9 %shard_map.95 = (bf16[64,512]{1,0:T(8,128)(2,1)}, f32[1,64]{1,0:T(1,128)}) custom-call(bf16[64,4096]{1,0:T(8,128)(2,1)} %b_ref.1, bf16[64,4096]{1,0:T(8,128)(2,1)} %c_ref.1, s32[16,1,512]{2,1,0:T(1,128)} %bitcast.11, s32[16,1,512]{2,1,0:T(1,128)} %k_ref.1, f32[16,1,512]{2,1,0:T(1,128)} %bitcast.12, bf16[256,128]{1,0:T(8,128)(2,1)} %bitcast.10, ...), custom_call_target="tpu_custom_call" | custom-call | tf_op jit(solution)/shard_map/pallas_call | solution.py:318
  57.5 0.0 copy-start
  57.5 1.5 %copy.12 = bf16[64,512]{1,0:T(8,128)(2,1)} copy(bf16[64,512]{1,0:T(8,128)(2,1)} %get-tuple-element.8) | data formatting | bytes 131072
  59.0 0.0 copy-done
  59.0 0.5 copy.13
Async XLA Ops:
  57.5 1.5 %copy-start = (f32[1,64]{1,0:T(1,128)S(1)}, f32[1,64]{1,0:T(1,128)}, u32[]{:S(2)}) copy-start(f32[1,64]{1,0:T(1,128)} %get-tuple-element.5) | copy-start | bytes 772
